TPU v7x, 32 devices: a whole 2x2x4 slice. The times are simulated.
32 devices in a mesh: data: 32 (over z, y, x, core).
Axes of the slice: x: 2, y: 2, z: 4, core: 2. Of those that a mesh axis runs over, the one named last changes fastest.
Arguments:
- x_in: bfloat16 [131072, 768], P('data')
- d_out: bfloat16 [131072, 768], P('data')
- w_stack: bfloat16 [4, 768, 768], replicated
- a_old: float32 [4, 768, 768], replicated
- s_old: float32 [4, 768, 768], replicated
- a_inv: float32 [4, 768, 768], replicated
- s_inv: float32 [4, 768, 768], replicated
Outputs:
- output 1: float32 [4, 768, 768], replicated
- output 2: float32 [4, 768, 768], replicated
- output 3: float32 [4, 768, 768], replicated
All inputs are finite; a program needn't handle non-finite values.
Results may differ from a plain program's by a relative error of at most 0.00117834.
Values are sent between devices in bfloat16 or wider.
A program may use at most 1 GiB of HBM per device.

v0:
```python
import jax
import jax.numpy as jnp
from jax import lax
from jax.sharding import PartitionSpec as P

RHO = 0.75
ERF_SCALE = 0.7071067811865476
PDF_SCALE = 0.3989422804014327


def gelu_fwd(z_val):
    return 0.5 * z_val * (1.0 + lax.erf(z_val * ERF_SCALE))


def gelu_slope(z_val):
    return 0.5 * (1.0 + lax.erf(z_val * ERF_SCALE)) + z_val * jnp.exp(-0.5 * z_val * z_val) * PDF_SCALE


def tok_gram(lhs_rows, rhs_rows):
    return lax.dot_general(lhs_rows, rhs_rows, (((0,), (0,)), ((), ())), preferred_element_type=jnp.float32)


def times_wt(g_rows, w_mat):
    return lax.dot_general(g_rows, w_mat, (((1,), (1,)), ((), ())), preferred_element_type=jnp.float32)


def precondition(a_inv, w_grad, s_inv):
    left_mul = jnp.einsum("lij,ljk->lik", a_inv, w_grad, precision=lax.Precision.HIGHEST, preferred_element_type=jnp.float32)
    return jnp.einsum("lij,ljk->lik", left_mul, s_inv, precision=lax.Precision.HIGHEST, preferred_element_type=jnp.float32)


def solution(mesh):
    group_size = mesh.shape["data"]

    def local_step(x_loc, dy_loc, w_stack, a_old, s_old, a_inv, s_inv):
        layers = w_stack.shape[0]
        half_rows = x_loc.shape[0] // 2
        tokens = x_loc.shape[0] * group_size
        a_acc = [None] * layers
        s_acc = [None] * layers
        w_acc = [None] * layers
        for micro_idx in range(2):
            lo_row = micro_idx * half_rows
            h_cur = x_loc[lo_row:lo_row + half_rows]
            layer_in = []
            pre_act = []
            for layer_idx in range(layers):
                layer_in.append(h_cur)
                a_part = tok_gram(h_cur, h_cur)
                a_acc[layer_idx] = a_part if micro_idx == 0 else a_acc[layer_idx] + a_part
                z_cur = jnp.dot(h_cur, w_stack[layer_idx], preferred_element_type=jnp.float32).astype(jnp.bfloat16)
                pre_act.append(z_cur)
                if layer_idx < layers - 1:
                    h_cur = gelu_fwd(z_cur.astype(jnp.float32)).astype(jnp.bfloat16)
            g_cur = dy_loc[lo_row:lo_row + half_rows]
            for layer_idx in reversed(range(layers)):
                if layer_idx < layers - 1:
                    g_cur = (dh_cur.astype(jnp.float32) * gelu_slope(pre_act[layer_idx].astype(jnp.float32))).astype(jnp.bfloat16)
                s_part = tok_gram(g_cur, g_cur)
                w_part = tok_gram(layer_in[layer_idx], g_cur)
                s_acc[layer_idx] = s_part if micro_idx == 0 else s_acc[layer_idx] + s_part
                w_acc[layer_idx] = w_part if micro_idx == 0 else w_acc[layer_idx] + w_part
                if layer_idx > 0:
                    dh_cur = times_wt(g_cur, w_stack[layer_idx]).astype(jnp.bfloat16)
        a_sum, s_sum, w_sum = lax.psum((jnp.stack(a_acc), jnp.stack(s_acc), jnp.stack(w_acc)), "data")
        a_new = RHO * a_old + (1.0 - RHO) * (a_sum / tokens)
        s_new = RHO * s_old + (1.0 - RHO) * (s_sum / tokens)
        u_stack = precondition(a_inv, w_sum / tokens, s_inv)
        return u_stack, a_new, s_new

    row_spec = P("data", None)
    full_spec = P()
    return jax.shard_map(local_step, mesh=mesh, in_specs=(row_spec, row_spec, full_spec, full_spec, full_spec, full_spec, full_spec), out_specs=(full_spec, full_spec, full_spec), check_vma=False)
```

profile of v0, /device:TPU:0, one launch (start us, length us, event | category | flops | bytes accessed | tf_op | source)
XLA Modules:
  0.0 712.5 jit_solution(7537822555252090921)
XLA Ops:
  7.2 7.1 fusion.57
  14.3 5.6 fusion.30
  33.7 5.1 fusion.21
  42.9 8.7 %fusion.112 = f32[768,768]{1,0:T(8,128)} fusion(f32[2048,768]{1,0:T(8,128)} %get-tuple-element.16, bf16[2048,768]{1,0:T(8,128)(2,1)S(1)} %get-tuple-element.17), kind=kOutput, calls=%fused_computation.161 | convolution fusion | flops 2422210560 | bytes 11796480 | tf_op jit(solution)/shard_map/dot_general | solution.py:20
  51.6 6.7 fusion.26
  58.3 7.1 fusion.116
  69.6 4.5 fusion.19
  86.5 4.6 fusion.48
  92.8 5.6 fusion.64
  98.4 7.0 fusion.53
  105.4 5.7 add_bitcast_fusion.7
  111.0 5.5 add_bitcast_fusion
  122.1 6.6 fusion.10
  132.8 9.9 %add_bitcast_fusion.4 = f32[1,768,768]{2,1,0:T(8,128)S(1)} fusion(f32[768,768]{1,0:T(8,128)} %fusion.112, f32[2048,768]{1,0:T(8,128)} %get-tuple-element.10, bf16[2048,768]{1,0:T(8,128)(2,1)} %copy-done.7), kind=kOutput, calls=%fused_computation.128 | convolution fusion | flops 2422800384 | bytes 14155776 | tf_op jit(solution)/shard_map/dot_general | solution.py:20
  142.7 7.5 %add_bitcast_fusion.8 = f32[1,768,768]{1,2,0:T(8,128)S(1)} fusion(f32[768,768]{0,1:T(8,128)S(1)} %fusion.64, bf16[4096,768]{1,0:T(8,128)(2,1)} %param.8, f32[2048,768]{1,0:T(8,128)} %get-tuple-element.16, bf16[2048,768]{1,0:T(8,128)(2,1)} %copy-done.4), kind=kOutput, calls=%fused_computation.132 | convolution fusion | flops 2422800384 | bytes 17301504 | tf_op jit(solution)/shard_map/dot_general | solution.py:20
  154.6 7.3 %fusion.46 = bf16[2048,768]{1,0:T(8,128)(2,1)S(1)} fusion(bf16[2048,768]{1,0:T(8,128)(2,1)} %get-tuple-element.9, bf16[2048,768]{1,0:T(8,128)(2,1)S(1)} %fusion.53, bf16[4,768,768]{2,1,0:T(8,128)(2,1)} %param.9), kind=kOutput, calls=%fused_computation.81 | convolution fusion | flops 2436366336 | bytes 10616832 | tf_op jit(solution)/shard_map/dot_general | solution.py:24
  164.5 4.5 add_bitcast_fusion.10
  169.1 7.5 %fusion.37 = bf16[2048,768]{1,0:T(8,128)(2,1)S(1)} fusion(bf16[2048,768]{1,0:T(8,128)(2,1)} %get-tuple-element.7, bf16[2048,768]{1,0:T(8,128)(2,1)S(1)} %fusion.46, bf16[4,768,768]{2,1,0:T(8,128)(2,1)} %param.9), kind=kOutput, calls=%fused_computation.72 | convolution fusion | flops 2436366336 | bytes 10616832 | tf_op jit(solution)/shard_map/dot_general | solution.py:24
  179.4 4.7 fusion.59
  186.9 4.6 add_bitcast_fusion.11
  203.7 431.6 %all-reduce.3.cloned.1.call-done = (f32[4,768,768]{1,2,0:T(8,128)}, f32[4,768,768]{2,1,0:T(8,128)}, f32[4,768,768]{2,1,0:T(8,128)}) async-done(((f32[4,768,768]{1,2,0:T(8,128)}, f32[4,768,768]{2,1,0:T(8,128)}, f32[4,768,768]{2,1,0:T(8,128)}), (f32[4,768,768]{1,2,0:T(8,128)}, f32[4,768,768]{2,1,0:T(8,128)}, f32[4,768,768]{2,1,0:T(8,128)})) %all-reduce.3.cloned.1.call-update) | async-done | bytes 28311568 | tf_op jit(solution)/shard_map/psum | solution.py:65
  635.3 25.9 %fusion = f32[4,768,768]{1,2,0:T(8,128)S(1)} fusion(f32[4,768,768]{2,1,0:T(8,128)} %param.12, f32[4,768,768]{1,2,0:T(8,128)} %get-tuple-element.3), kind=kOutput, calls=%fused_computation.35 | convolution fusion | flops 21745631232 | bytes 28311552 | tf_op jit(solution)/shard_map/lij,ljk->lik/dot_general | solution.py:28
  661.2 26.5 %fusion.117 = f32[4,768,768]{2,1,0:T(8,128)} fusion(f32[4,768,768]{1,2,0:T(8,128)S(1)} %fusion, f32[4,768,768]{2,1,0:T(8,128)} %param.13), kind=kOutput, calls=%fused_computation.164 | convolution fusion | flops 21743271936 | bytes 28311552 | tf_op jit(solution)/shard_map/lij,ljk->lik/dot_general | solution.py:29
  687.8 17.6 %multiply_add_fusion = (f32[4,768,768]{2,1,0:T(8,128)}, f32[4,768,768]{2,1,0:T(8,128)}) fusion(f32[4,768,768]{2,1,0:T(8,128)} %get-tuple-element.5, f32[4,768,768]{2,1,0:T(8,128)S(1)} %bitcast.108, f32[4,768,768]{2,1,0:T(8,128)} %get-tuple-element.4, f32[4,768,768]{2,1,0:T(8,128)} %param.10), kind=kLoop, calls=%fused_computation.33 | loop fusion | flops 14155776 | bytes 56623104 | tf_op jit(solution)/shard_map/add | solution.py:67
  (66 shorter events, 70.4 us)
Async XLA Ops:
  7.2 628.1 %all-reduce.3.cloned.1.call-start = ((), (), s32[]{:S(2)}) async-start(), calls=%async_computation | async-start | bytes 56623104 | tf_op jit(solution)/shard_map/psum | solution.py:65
  7.2 7.1 copy-start.3
  7.2 12.7 %slice-start.5 = ((s8[4718592]{0:T(1024)(128)(4,1)}), s8[4194304]{0:T(1024)(128)(4,1)S(1)}, s32[]{:S(2)}) async-start(s8[4718592]{0:T(1024)(128)(4,1)} %bitcast.111), calls=%async_computation.6 | async-start | bytes 8388608
  14.3 5.6 slice-start.6
  31.0 2.7 copy-start.10
  31.0 7.8 %slice-start.3 = ((s8[6291456]{0:T(1024)(128)(4,1)}), s8[4194304]{0:T(1024)(128)(4,1)S(1)}, s32[]{:S(2)}) async-start(s8[6291456]{0:T(1024)(128)(4,1)} %bitcast.109), calls=%async_computation.4 | async-start | bytes 8388608
  33.7 5.1 slice-start.4
  38.9 12.8 %copy-start.4 = (bf16[2048,768]{1,0:T(8,128)(2,1)}, bf16[2048,768]{1,0:T(8,128)(2,1)S(1)}, u32[]{:S(2)}) copy-start(bf16[2048,768]{1,0:T(8,128)(2,1)S(1)} %get-tuple-element.17) | copy-start | bytes 9437188
  58.3 7.1 copy-start.11
  65.4 4.2 copy-start.12
  74.0 4.1 copy-start.8
  91.1 1.7 copy-start.7
  98.4 7.0 copy-start.5
  105.4 5.7 copy-start.6
  119.2 2.7 copy-start.9
  119.2 2.8 copy-start.13
  154.5 7.3 %copy-start.1 = (f32[768,768]{1,0:T(8,128)S(1)}, f32[768,768]{1,0:T(8,128)}, u32[]{:S(2)}) copy-start(f32[768,768]{1,0:T(8,128)} %fusion.122) | copy-start | bytes 7077892
  169.1 7.5 %copy-start = (f32[768,768]{1,0:T(8,128)S(1)}, f32[768,768]{1,0:T(8,128)}, u32[]{:S(2)}) copy-start(f32[768,768]{1,0:T(8,128)} %fusion.121) | copy-start | bytes 7077892
  179.4 4.8 copy-start.2
  635.3 52.5 %slice-start = ((s8[9437184]{0:T(1024)(128)(4,1)}), s8[4194304]{0:T(1024)(128)(4,1)S(1)}, s32[]{:S(2)}) async-start(s8[9437184]{0:T(1024)(128)(4,1)} %bitcast.107), calls=%async_computation.1 | async-start | bytes 8388608
  635.3 52.5 %slice-start.1 = ((s8[9437184]{0:T(1024)(128)(4,1)}), s8[4194304]{0:T(1024)(128)(4,1)S(1)}, s32[]{:S(2)}) async-start(s8[9437184]{0:T(1024)(128)(4,1)} %bitcast.107), calls=%async_computation.2 | async-start | bytes 8388608
  661.2 26.6 %slice-start.2 = ((s8[9437184]{0:T(1024)(128)(4,1)}), s8[1048576]{0:T(1024)(128)(4,1)S(1)}, s32[]{:S(2)}) async-start(s8[9437184]{0:T(1024)(128)(4,1)} %bitcast.107), calls=%async_computation.3 | async-start | bytes 2097152
Sparse Core Ops, SparseCore 0:
  203.8 431.4 all-reduce.2
where the time goes:
time: 721 us; the launch traced here: 712 us
  waiting for transfers between devices  432 us (60%)
  matrix products  234 us (32%)
  other arithmetic  29.8 us (4%)
  between operations  14.6 us (2%)
    psum x1, waiting for transfers between devices, local_step(): lax.psum((jnp.stack(a_acc), jnp.stack(s_acc), jnp.stack(w_acc)), 'data')  432 us
    dot_general x24, matrix products, tok_gram(): lax.dot_general(lhs_rows, rhs_rows, (((0,), (0,)), ((), ())), preferred_e...  115 us
    dot_general x6, matrix products, times_wt(): lax.dot_general(g_rows, w_mat, (((1,), (1,)), ((), ())), preferred_elemen...  39.6 us
    dot_general x6, matrix products, local_step(): jnp.dot(h_cur, w_stack[layer_idx], preferred_element_type=jnp.float32)  27.8 us
    dot_general x1, matrix products, precondition(): jnp.einsum('lij,ljk->lik', left_mul, s_inv, precision=lax.Precision.HIGHE...  26.5 us
    dot_general x1, matrix products, precondition(): jnp.einsum('lij,ljk->lik', a_inv, w_grad, precision=lax.Precision.HIGHEST...  25.9 us
    add x1, other arithmetic, local_step(): s_new = RHO * s_old + (1.0 - RHO) * (s_sum / tokens)  17.6 us
  transfers between devices with their start and end apart: 1, of which 1 were waited for; matrix products, arithmetic and copies ran while one was open for 0% of the time, Pallas kernels for 0%

commit v1 on v0

v1 whole, which is shorter than its diff:
```python
import functools

import jax
import jax.numpy as jnp
from jax import lax
from jax.experimental import pallas as pl
from jax.experimental.pallas import tpu as pltpu
from jax.sharding import PartitionSpec as P

RHO = 0.75
ERF_SCALE = 0.7071067811865476
PDF_SCALE = 0.3989422804014327

D = 768
BLK = 256
LAYERS = 4
UNIT = 256
MATS = 12
UNITS = 28
HALVINGS = 4
COPIES = 2 * HALVINGS + 1
RROWS = 256
MESH = pl.DeviceIdType.MESH
ORDERS = ((1, 2, 4, 8, 16), (1, 4, 2, 8, 16), (1, 8, 16, 2, 4))
CHUNKS = 4
DN0 = (((0,), (0,)), ((), ()))


def gelu_fwd(z_val):
    return 0.5 * z_val * (1.0 + lax.erf(z_val * ERF_SCALE))


def gelu_slope(z_val):
    return 0.5 * (1.0 + lax.erf(z_val * ERF_SCALE)) + z_val * jnp.exp(-0.5 * z_val * z_val) * PDF_SCALE


def times_wt(g_rows, w_mat):
    return lax.dot_general(g_rows, w_mat, (((1,), (1,)), ((), ())), preferred_element_type=jnp.float32)


def half_of(step):
    return 128 >> step


def land_of(step):
    return 256 - (256 >> step)


def reduce_kernel(inv_tokens, x, h1, h2, h3, g1, g2, g3, dy, ainv, sinv,
                  sym_out, u_out,
                  pay, rbuf, lbuf, gbuf, av, sv, ub,
                  ssem, rsem, fsem, lsem, gsem, isem, usem, osem):
    me = lax.axis_index("data")
    tok = x.shape[0]
    chunk = tok // CHUNKS
    acts = (x, h1, h2, h3)
    grads = (g1, g2, g3, dy)

    def bit(mask):
        return lax.rem(lax.div(me, mask), 2)

    def peer(mask):
        return me + mask * (1 - 2 * bit(mask))

    barrier = pltpu.get_barrier_semaphore()
    for mask in ORDERS[0]:
        pl.semaphore_signal(barrier, inc=1, device_id=(peer(mask),), device_id_type=MESH)
    pl.semaphore_wait(barrier, 5)

    def offset(order, step):
        off = 0
        for s in range(step):
            off = off + bit(order[s]) * half_of(s)
        return off

    def base_of(m):
        late = lax.div(m + 8, 12)
        return 3 * m - late * (m - 4)

    def rows_at(ref, start, size):
        return ref.at[pl.ds(pl.multiple_of(start, 8), size), :]

    def scatter_copy(m, j, step):
        order = ORDERS[j]
        unit = base_of(m) + j
        half = half_of(step)
        b = bit(order[step])
        src = unit * UNIT + offset(order, step) + (1 - b) * half
        return pltpu.make_async_remote_copy(
            src_ref=rows_at(pay, src, half),
            dst_ref=rows_at(rbuf, unit * RROWS + land_of(step), half),
            send_sem=ssem.at[m, j, step], recv_sem=rsem.at[m, j, step],
            device_id=(peer(order[step]),), device_id_type=MESH)

    def exchange_copy(m, j):
        order = ORDERS[j]
        unit = base_of(m) + j
        return pltpu.make_async_remote_copy(
            src_ref=rows_at(pay, unit * UNIT + offset(order, HALVINGS), 16),
            dst_ref=rows_at(rbuf, unit * RROWS + 240, 16),
            send_sem=ssem.at[m, j, HALVINGS], recv_sem=rsem.at[m, j, HALVINGS],
            device_id=(peer(order[HALVINGS]),), device_id_type=MESH)

    def gather_copy(m, j, step):
        order = ORDERS[j]
        unit = base_of(m) + j
        half = half_of(step)
        row = unit * UNIT + offset(order, step + 1)
        return pltpu.make_async_remote_copy(
            src_ref=rows_at(pay, row, half),
            dst_ref=rows_at(pay, row, half),
            send_sem=ssem.at[m, j, HALVINGS + 1 + step], recv_sem=rsem.at[m, j, HALVINGS + 1 + step],
            device_id=(peer(order[step]),), device_id_type=MESH)

    def give_back(m, j, step):
        pl.semaphore_signal(fsem.at[m, j, step], inc=1, device_id=(peer(ORDERS[j][step]),), device_id_type=MESH)

    def gather_start(m, j, step):
        pl.semaphore_wait(fsem.at[m, j, step], 1)
        gather_copy(m, j, step).start()

    def add_landed(m, j, step):
        order = ORDERS[j]
        unit = base_of(m) + j
        half = half_of(step) if step < HALVINGS else 16
        keep = unit * UNIT + offset(order, min(step + 1, HALVINGS))
        land = unit * RROWS + land_of(step)
        piece = min(half, 32)

        def one(i, carry):
            a = pl.ds(pl.multiple_of(keep + i * piece, 8), piece)
            c = pl.ds(pl.multiple_of(land + i * piece, 8), piece)
            pay[a, :] = pay[a, :] + rbuf[c, :]
            return carry

        if half == piece:
            one(0, 0)
        else:
            lax.fori_loop(0, half // piece, one, 0)

    def stage(k, m, j):
        if k <= HALVINGS:
            scatter_copy(m, j, k - 1).wait()
            give_back(m, j, k - 1)
            add_landed(m, j, k - 1)
            if k < HALVINGS:
                scatter_copy(m, j, k).start()
            else:
                exchange_copy(m, j).start()
        elif k == HALVINGS + 1:
            exchange_copy(m, j).wait()
            add_landed(m, j, HALVINGS)
            gather_start(m, j, HALVINGS - 1)
        else:
            step = COPIES - k
            gather_copy(m, j, step).wait()
            if step > 0:
                gather_start(m, j, step - 1)

    def wait_left(kc, slot):
        pltpu.make_async_copy(x.at[pl.ds(kc * chunk, chunk), :], lbuf.at[slot], lsem.at[slot]).wait()

    def wait_right(kc, slot):
        pltpu.make_async_copy(dy.at[pl.ds(kc * chunk, chunk), :], gbuf.at[slot], gsem.at[slot]).wait()

    def load(m, kc, slot):
        rows = pl.ds(kc * chunk, chunk)
        for i in range(MATS):
            if i < 4:
                left, right = acts[3 - i], grads[3 - i]
            else:
                left, right = (acts + grads)[i - 4], None

            @pl.when(m == i)
            def _(left=left, right=right):
                pltpu.make_async_copy(left.at[rows, :], lbuf.at[slot], lsem.at[slot]).start()
                if right is not None:
                    pltpu.make_async_copy(right.at[rows, :], gbuf.at[slot], gsem.at[slot]).start()

    def put(first, row, rows, c0, cols, val):
        a = pl.ds(pl.multiple_of(row, 8), rows)
        if first:
            pay[a, c0:c0 + cols] = val
        else:
            pay[a, c0:c0 + cols] = pay[a, c0:c0 + cols] + val

    def gram_dw(m):
        row = base_of(m) * UNIT
        for kc in range(CHUNKS):
            slot = kc % 2
            wait_left(kc, slot)
            wait_right(kc, slot)
            if kc + 1 < CHUNKS:
                load(m, kc + 1, 1 - slot)
            for j in range(3):
                val = lax.dot_general(lbuf[slot, :, j * BLK:(j + 1) * BLK], gbuf[slot], DN0,
                                      preferred_element_type=jnp.float32)
                put(kc == 0, row + j * UNIT, UNIT, 0, D, val)

    def gram_sym(m):
        row = base_of(m) * UNIT
        for kc in range(CHUNKS):
            slot = kc % 2
            wait_left(kc, slot)
            if kc + 1 < CHUNKS:
                load(m, kc + 1, 1 - slot)
            for j, (unit, c0) in enumerate(((0, 0), (1, 0), (1, 2 * BLK))):
                cols = D - j * BLK
                val = lax.dot_general(lbuf[slot, :, j * BLK:(j + 1) * BLK], lbuf[slot, :, j * BLK:], DN0,
                                      preferred_element_type=jnp.float32)
                put(kc == 0, row + unit * UNIT, UNIT, c0, cols, val)

    def inv_copies(m):
        layer = 3 - m
        return (pltpu.make_async_copy(ainv.at[layer], av, isem.at[0]),
                pltpu.make_async_copy(sinv.at[layer], sv, isem.at[1]))

    def u_copy(m):
        return pltpu.make_async_copy(ub, u_out.at[3 - m], usem.at[0])

    def precondition(m):
        ac, sc = inv_copies(m)
        ac.wait()
        sc.wait()

        @pl.when(m > 0)
        def _():
            u_copy(m - 1).wait()

        dw = pl.ds(pl.multiple_of(3 * m * UNIT, 8), D)

        def strip(i, carry):
            a = pl.ds(pl.multiple_of(i * BLK, 8), BLK)
            left = jnp.dot(av[a, :], pay[dw, :] * inv_tokens, precision=lax.Precision.HIGHEST,
                           preferred_element_type=jnp.float32)
            ub[a, :] = jnp.dot(left, sv[...], precision=lax.Precision.HIGHEST,
                               preferred_element_type=jnp.float32)
            return carry

        lax.fori_loop(0, 3, strip, 0)
        u_copy(m).start()

    def sym_copy(m):
        return pltpu.make_async_copy(rows_at(pay, base_of(m) * UNIT, 2 * UNIT), sym_out.at[m - 4], osem.at[m - 4])

    load(0, 0, 0)

    def tick(t, carry):
        for k in range(COPIES, 0, -1):
            m = t - k

            @pl.when(jnp.logical_and(m >= 0, m < MATS))
            def _(k=k, m=m):
                stage(k, m, 0)
                stage(k, m, 1)

                @pl.when(m < 4)
                def _():
                    stage(k, m, 2)
                    if k == COPIES - 1:
                        for c in inv_copies(m):
                            c.start()
                    if k == COPIES:
                        precondition(m)

                if k == COPIES:
                    @pl.when(m >= 4)
                    def _():
                        sym_copy(m).start()

        @pl.when(t < MATS)
        def _():
            @pl.when(t < 4)
            def _():
                gram_dw(t)

            @pl.when(t >= 4)
            def _():
                gram_sym(t)

            load(t + 1, 0, 0)
            scatter_copy(t, 0, 0).start()
            scatter_copy(t, 1, 0).start()

            @pl.when(t < 4)
            def _():
                scatter_copy(t, 2, 0).start()

        return carry

    lax.fori_loop(0, MATS + COPIES, tick, 0)
    u_copy(3).wait()

    def finish(m, carry):
        sym_copy(m).wait()
        return carry

    lax.fori_loop(4, MATS, finish, 0)


def reduce_all(arrays, ainv, sinv, tokens):
    any_spec = pl.BlockSpec(memory_space=pl.ANY)
    tok = arrays[0].shape[0]
    f32, bf16 = jnp.float32, jnp.bfloat16
    flops = 2 * tok * D * D * 10 + 8 * 12 * D ** 3
    return pl.pallas_call(
        functools.partial(reduce_kernel, 1.0 / tokens),
        out_shape=(jax.ShapeDtypeStruct((8, 2 * UNIT, D), f32), jax.ShapeDtypeStruct((LAYERS, D, D), f32)),
        in_specs=[any_spec] * 10,
        out_specs=(any_spec, any_spec),
        scratch_shapes=[
            pltpu.VMEM((UNITS * UNIT, D), f32),
            pltpu.VMEM((UNITS * RROWS, D), f32),
            pltpu.VMEM((2, tok // CHUNKS, D), bf16),
            pltpu.VMEM((2, tok // CHUNKS, D), bf16),
            pltpu.VMEM((D, D), f32),
            pltpu.VMEM((D, D), f32),
            pltpu.VMEM((D, D), f32),
            pltpu.SemaphoreType.DMA((MATS, 3, COPIES)),
            pltpu.SemaphoreType.DMA((MATS, 3, COPIES)),
            pltpu.SemaphoreType.REGULAR((MATS, 3, HALVINGS)),
            pltpu.SemaphoreType.DMA((2,)),
            pltpu.SemaphoreType.DMA((2,)),
            pltpu.SemaphoreType.DMA((2,)),
            pltpu.SemaphoreType.DMA((1,)),
            pltpu.SemaphoreType.DMA((8,)),
        ],
        compiler_params=pltpu.CompilerParams(collective_id=0, has_side_effects=True, vmem_limit_bytes=66 * 1000 * 1000),
        cost_estimate=pl.CostEstimate(flops=flops, bytes_accessed=8 * tok * D * 4, transcendentals=0),
        name="token_sums_reduced",
    )(*arrays, ainv, sinv)


def fold_kernel(scale, pa, ps, ao, so, an, sn):
    strip = pl.program_id(1)
    for packed, old, new in ((pa, ao, an), (ps, so, sn)):
        @pl.when(strip == 0)
        def _(packed=packed, old=old, new=new):
            new[0] = RHO * old[0] + scale * packed[0, 0:BLK, :]

        @pl.when(strip == 1)
        def _(packed=packed, old=old, new=new):
            new[0, :, 0:BLK] = RHO * old[0, :, 0:BLK] + scale * packed[0, 0:BLK, BLK:2 * BLK].T
            new[0, :, BLK:] = RHO * old[0, :, BLK:] + scale * packed[0, BLK:, 0:2 * BLK]

        @pl.when(strip == 2)
        def _(packed=packed, old=old, new=new):
            new[0, :, 0:BLK] = RHO * old[0, :, 0:BLK] + scale * packed[0, 0:BLK, 2 * BLK:].T
            new[0, :, BLK:2 * BLK] = RHO * old[0, :, BLK:2 * BLK] + scale * packed[0, BLK:, BLK:2 * BLK].T
            new[0, :, 2 * BLK:] = RHO * old[0, :, 2 * BLK:] + scale * packed[0, BLK:, 2 * BLK:]


def fold(packed, a_old, s_old, tokens):
    f32 = jnp.float32
    pack_a = pl.BlockSpec((1, 2 * UNIT, D), lambda l, i: (l, 0, 0))
    pack_s = pl.BlockSpec((1, 2 * UNIT, D), lambda l, i: (l + LAYERS, 0, 0))
    strip = pl.BlockSpec((1, BLK, D), lambda l, i: (l, i, 0))
    shape = jax.ShapeDtypeStruct((LAYERS, D, D), f32)
    return pl.pallas_call(
        functools.partial(fold_kernel, (1.0 - RHO) / tokens),
        out_shape=(shape, shape),
        grid=(LAYERS, 3),
        in_specs=[pack_a, pack_s, strip, strip],
        out_specs=(strip, strip),
        name="fold_factors",
    )(packed, packed, a_old, s_old)


def solution(mesh):
    group_size = mesh.shape["data"]

    def local_step(x_loc, dy_loc, w_stack, a_old, s_old, a_inv, s_inv):
        layers = w_stack.shape[0]
        tokens = x_loc.shape[0] * group_size
        acts = [x_loc]
        pre = []
        for i in range(layers - 1):
            z = jnp.dot(acts[-1], w_stack[i], preferred_element_type=jnp.float32).astype(jnp.bfloat16)
            pre.append(z)
            acts.append(gelu_fwd(z.astype(jnp.float32)).astype(jnp.bfloat16))
        grads = [None] * layers
        grads[-1] = dy_loc
        for i in reversed(range(layers - 1)):
            dh = times_wt(grads[i + 1], w_stack[i + 1]).astype(jnp.bfloat16)
            grads[i] = (dh.astype(jnp.float32) * gelu_slope(pre[i].astype(jnp.float32))).astype(jnp.bfloat16)
        packed, u_stack = reduce_all(acts + grads, a_inv, s_inv, tokens)
        a_new, s_new = fold(packed, a_old, s_old, tokens)
        return u_stack, a_new, s_new

    row_spec = P("data", None)
    full_spec = P()
    return jax.shard_map(local_step, mesh=mesh, in_specs=(row_spec, row_spec, full_spec, full_spec, full_spec, full_spec, full_spec), out_specs=(full_spec, full_spec, full_spec), check_vma=False)
```

time: 721 us -> 330 us (0.46); the launches traced: 712 us -> 329 us
  waiting for transfers between devices: 432 us -> 0 us
  Pallas kernels: 0 us -> 260 us
  matrix products: 234 us -> 57.7 us
  other arithmetic: 29.8 us -> 0.01 us
  between operations: 14.6 us -> 0.76 us
  local copies, waits for them, and re-layouts: 1.91 us -> 10.7 us
    psum x1 -> x0, waiting for transfers between devices: 432 us -> none  [local_step(): lax.psum((jnp.stack(a_acc), jnp.stack(s_acc), jnp.stack(w_acc)), 'data')]
    pallas_call x0 -> x2, Pallas kernels: none -> 260 us  [the longest x1 240 us: reduce_all(): pl.pallas_call(functools.partial(reduce_kernel, 1.0 / tokens), out_shape=...]
    dot_general x32 -> x3, matrix products: 195 us -> 29.1 us  [local_step(): jnp.dot(acts[-1], w_stack[i], preferred_element_type=jnp.float32)]
    add x1 -> x0, other arithmetic: 17.6 us -> none  [local_step(): s_new = RHO * s_old + (1.0 - RHO) * (s_sum / tokens)]
    another operation x3 -> x0, other arithmetic: 12.2 us -> none  [the longest x1 4.07 us: local_step(): jnp.stack(a_acc)]
    dot_general x6 -> x3, matrix products: 39.6 us -> 28.6 us  [times_wt(): lax.dot_general(g_rows, w_mat, (((1,), (1,)), ((), ())), preferred_elemen...]
    unnamed x42 -> x17, local copies, waits for them, and re-layouts: 1.91 us -> 10.7 us
  transfers between devices with their start and end apart: 1 -> 0, of which waited for: 1 -> 0; matrix products, arithmetic and copies ran while one was open for 0% -> 0% of each run, Pallas kernels for 0% -> 0%
where the time goes in v1:
time: 330 us; the launch traced here: 329 us
  Pallas kernels  260 us (79%)
  matrix products  57.7 us (17%)
  local copies, waits for them, and re-layouts  10.7 us (3%)
    pallas_call x1, Pallas kernels, reduce_all(): pl.pallas_call(functools.partial(reduce_kernel, 1.0 / tokens), out_shape=...  240 us
    dot_general x3, matrix products, local_step(): jnp.dot(acts[-1], w_stack[i], preferred_element_type=jnp.float32)  29.1 us
    dot_general x3, matrix products, times_wt(): lax.dot_general(g_rows, w_mat, (((1,), (1,)), ((), ())), preferred_elemen...  28.6 us
    pallas_call x1, Pallas kernels, fold(): pl.pallas_call(functools.partial(fold_kernel, (1.0 - RHO) / tokens), out_...  19.8 us
    unnamed x17, local copies, waits for them, and re-layouts  10.7 us

profile of v1, /device:TPU:0, one launch (start us, length us, event | category | flops | bytes accessed | tf_op | source)
XLA Modules:
  0.0 328.8 jit_solution(9342637318984999015)
XLA Ops:
  0.6 0.0 copy-start
  0.6 8.3 %fusion.1 = (bf16[4096,768]{1,0:T(8,128)(2,1)S(1)}, bf16[4096,768]{1,0:T(8,128)(2,1)S(1)}) fusion(bf16[4096,768]{1,0:T(8,128)(2,1)} %x.1, bf16[4,768,768]{2,1,0:T(8,128)(2,1)} %param.9), kind=kOutput, calls=%fused_computation.16 | convolution fusion | flops 4853858304 | bytes 20054016 | tf_op jit(solution)/shard_map/dot_general | solution.py:378
  8.9 0.0 copy-start.1
  9.0 0.0 copy-done
  9.0 0.0 slice-start
  9.0 9.8 %fusion.10 = (bf16[4096,768]{1,0:T(8,128)(2,1)}, bf16[4096,768]{1,0:T(8,128)(2,1)}) fusion(bf16[4096,768]{1,0:T(8,128)(2,1)S(1)} %get-tuple-element.11.h1, bf16[4,768,768]{2,1,0:T(8,128)(2,1)S(1)} %copy-done), kind=kOutput, calls=%fused_computation.25 | convolution fusion | flops 4853858304 | bytes 20054016 | tf_op jit(solution)/shard_map/dot_general | solution.py:378
  18.8 0.0 copy-done.1
  18.8 0.0 slice-start.1
  18.8 11.0 %fusion.19 = (bf16[4096,768]{1,0:T(8,128)(2,1)}, bf16[4096,768]{1,0:T(8,128)(2,1)}) fusion(bf16[4096,768]{1,0:T(8,128)(2,1)} %get-tuple-element.13.h2, bf16[4,768,768]{2,1,0:T(8,128)(2,1)S(1)} %copy-done), kind=kOutput, calls=%fused_computation.34 | convolution fusion | flops 4853858304 | bytes 20054016 | tf_op jit(solution)/shard_map/dot_general | solution.py:378
  29.8 0.0 slice-done
  29.8 0.0 slice-done.1
  29.8 0.0 slice-start.3
  29.8 10.1 %fusion.26.g3 = bf16[4096,768]{1,0:T(8,128)(2,1)S(1)} fusion(bf16[4096,768]{1,0:T(8,128)(2,1)} %get-tuple-element.16, bf16[4096,768]{1,0:T(8,128)(2,1)S(1)} %bitcast.35, bf16[4,768,768]{2,1,0:T(8,128)(2,1)S(1)} %copy-done), kind=kOutput, calls=%fused_computation.41 | convolution fusion | flops 4872732672 | bytes 20054016 | tf_op jit(solution)/shard_map/dot_general | solution.py:38
  39.9 0.0 slice-done.2
  39.9 0.0 slice-done.3
  39.9 0.0 copy-start.2
  39.9 8.8 %fusion.17.g2 = bf16[4096,768]{1,0:T(8,128)(2,1)S(1)} fusion(bf16[4096,768]{1,0:T(8,128)(2,1)S(1)} %bitcast.37, bf16[4096,768]{1,0:T(8,128)(2,1)S(1)} %fusion.26.g3, bf16[4,768,768]{2,1,0:T(8,128)(2,1)S(1)} %copy-done), kind=kOutput, calls=%fused_computation.32 | convolution fusion | flops 4872732672 | bytes 20054016 | tf_op jit(solution)/shard_map/dot_general | solution.py:38
  48.7 0.0 copy-done.2
  48.8 0.0 copy-start.3
  48.8 2.6 copy-done.3
  51.4 9.7 %fusion.8.g1 = bf16[4096,768]{1,0:T(8,128)(2,1)} fusion(bf16[4096,768]{1,0:T(8,128)(2,1)S(1)} %get-tuple-element.12, bf16[4096,768]{1,0:T(8,128)(2,1)S(1)} %fusion.17.g2, bf16[4,768,768]{2,1,0:T(8,128)(2,1)S(1)} %copy-done), kind=kOutput, calls=%fused_computation.23 | convolution fusion | flops 4872732672 | bytes 20054016 | tf_op jit(solution)/shard_map/dot_general | solution.py:38
  61.1 239.9 %token_sums_reduced.1 = (f32[8,512,768]{2,1,0:T(8,128)}, f32[4,768,768]{2,1,0:T(8,128)}) custom-call(bf16[4096,768]{1,0:T(8,128)(2,1)} %x.1, bf16[4096,768]{1,0:T(8,128)(2,1)} %copy-done.1, bf16[4096,768]{1,0:T(8,128)(2,1)} %get-tuple-element.13.h2, bf16[4096,768]{1,0:T(8,128)(2,1)} %get-tuple-element.15.h3, bf16[4096,768]{1,0:T(8,128)(2,1)} %fusion.8.g1, ...), custom_call_target="tpu_custom_call" | custom-call | flops 91804925952 | bytes 100663296 | tf_op jit(solution)/shard_map/token_sums_reduced/pallas_call | solution.py:306
  301.0 19.8 %fold_factors.1 = (f32[4,768,768]{2,1,0:T(8,128)}, f32[4,768,768]{2,1,0:T(8,128)}) custom-call(f32[8,512,768]{2,1,0:T(8,128)} %get-tuple-element.8.pa.ps, f32[8,512,768]{2,1,0:T(8,128)} %get-tuple-element.8.pa.ps, f32[4,768,768]{2,1,0:T(8,128)} %ao.1, f32[4,768,768]{2,1,0:T(8,128)} %so.1), custom_call_target="tpu_custom_call" | custom-call | tf_op jit(solution)/shard_map/fold_factors/pallas_call | solution.py:359
  320.8 8.0 %copy.11 = f32[4,768,768]{2,1,0:T(8,128)} copy(f32[4,768,768]{2,1,0:T(8,128)} %get-tuple-element.20) | data formatting | bytes 18874368
  (3 shorter events, 0.0 us)
Async XLA Ops:
  0.6 8.3 %copy-start = (bf16[4,768,768]{2,1,0:T(8,128)(2,1)S(1)}, bf16[4,768,768]{2,1,0:T(8,128)(2,1)}, u32[]{:S(2)}) copy-start(bf16[4,768,768]{2,1,0:T(8,128)(2,1)} %param.9) | copy-start | bytes 14155780
  8.9 9.8 %copy-start.1 = (bf16[4096,768]{1,0:T(8,128)(2,1)}, bf16[4096,768]{1,0:T(8,128)(2,1)S(1)}, u32[]{:S(2)}) copy-start(bf16[4096,768]{1,0:T(8,128)(2,1)S(1)} %get-tuple-element.11.h1) | copy-start | bytes 18874372
  9.0 20.8 %slice-start = ((s8[6291456]{0:T(1024)(128)(4,1)}), s8[4194304]{0:T(1024)(128)(4,1)S(1)}, s32[]{:S(2)}) async-start(s8[6291456]{0:T(1024)(128)(4,1)} %bitcast.34), calls=%async_computation | async-start | bytes 8388608
  18.8 11.0 %slice-start.1 = ((s8[6291456]{0:T(1024)(128)(4,1)}), s8[2097152]{0:T(1024)(128)(4,1)S(1)}, s32[]{:S(2)}) async-start(s8[6291456]{0:T(1024)(128)(4,1)} %bitcast.34), calls=%async_computation.1 | async-start | bytes 4194304
  18.8 21.1 %slice-start.2 = ((s8[6291456]{0:T(1024)(128)(4,1)}), s8[4194304]{0:T(1024)(128)(4,1)S(1)}, s32[]{:S(2)}) async-start(s8[6291456]{0:T(1024)(128)(4,1)} %bitcast.36), calls=%async_computation.2 | async-start | bytes 8388608
  29.8 10.1 %slice-start.3 = ((s8[6291456]{0:T(1024)(128)(4,1)}), s8[2097152]{0:T(1024)(128)(4,1)S(1)}, s32[]{:S(2)}) async-start(s8[6291456]{0:T(1024)(128)(4,1)} %bitcast.36), calls=%async_computation.3 | async-start | bytes 4194304
  39.9 8.8 %copy-start.2 = (bf16[4096,768]{1,0:T(8,128)(2,1)}, bf16[4096,768]{1,0:T(8,128)(2,1)S(1)}, u32[]{:S(2)}) copy-start(bf16[4096,768]{1,0:T(8,128)(2,1)S(1)} %fusion.26.g3) | copy-start | bytes 18874372
  48.8 2.6 copy-start.3

commit v2 on v1

--- a/solution.py
+++ b/solution.py
@@ -15,6 +15,7 @@
 BLK = 256
 LAYERS = 4
 UNIT = 256
+HROWS = 384
 MATS = 12
 UNITS = 28
 HALVINGS = 4
@@ -23,6 +24,7 @@
 MESH = pl.DeviceIdType.MESH
 ORDERS = ((1, 2, 4, 8, 16), (1, 4, 2, 8, 16), (1, 8, 16, 2, 4))
 CHUNKS = 4
+LAG = (0, 1, 3, 5, 7, 9, 11, 13, 15, 16)
 DN0 = (((0,), (0,)), ((), ()))
 
 
@@ -49,7 +51,7 @@
 def reduce_kernel(inv_tokens, x, h1, h2, h3, g1, g2, g3, dy, ainv, sinv,
                   sym_out, u_out,
                   pay, rbuf, lbuf, gbuf, av, sv, ub,
-                  ssem, rsem, fsem, lsem, gsem, isem, usem, osem):
+                  ssem, rsem, fsem, lsem, gsem, isem, usem, ussem, ursem, osem):
     me = lax.axis_index("data")
     tok = x.shape[0]
     chunk = tok // CHUNKS
@@ -210,44 +212,56 @@
                                       preferred_element_type=jnp.float32)
                 put(kc == 0, row + unit * UNIT, UNIT, c0, cols, val)
 
+    own = pl.ds(pl.multiple_of(bit(1) * HROWS, 8), HROWS)
+
     def inv_copies(m):
         layer = 3 - m
-        return (pltpu.make_async_copy(ainv.at[layer], av, isem.at[0]),
+        return (pltpu.make_async_copy(ainv.at[layer, own, :], av, isem.at[0]),
                 pltpu.make_async_copy(sinv.at[layer], sv, isem.at[1]))
 
-    def u_copy(m):
-        return pltpu.make_async_copy(ub, u_out.at[3 - m], usem.at[0])
+    def u_copies(m):
+        dst = u_out.at[3 - m, own, :]
+        return (pltpu.make_async_copy(ub, dst, usem.at[0]),
+                pltpu.make_async_remote_copy(
+                    src_ref=ub, dst_ref=dst, send_sem=ussem.at[m], recv_sem=ursem.at[m],
+                    device_id=(peer(1),), device_id_type=MESH))
+
+    def u_left(m):
+        near, far = u_copies(m)
+        near.wait()
+        far.wait_send()
 
     def precondition(m):
-        ac, sc = inv_copies(m)
-        ac.wait()
-        sc.wait()
+        for c in inv_copies(m):
+            c.wait()
 
         @pl.when(m > 0)
         def _():
-            u_copy(m - 1).wait()
+            u_left(m - 1)
 
         dw = pl.ds(pl.multiple_of(3 * m * UNIT, 8), D)
-
-        def strip(i, carry):
-            a = pl.ds(pl.multiple_of(i * BLK, 8), BLK)
-            left = jnp.dot(av[a, :], pay[dw, :] * inv_tokens, precision=lax.Precision.HIGHEST,
-                           preferred_element_type=jnp.float32)
-            ub[a, :] = jnp.dot(left, sv[...], precision=lax.Precision.HIGHEST,
-                               preferred_element_type=jnp.float32)
-            return carry
-
-        lax.fori_loop(0, 3, strip, 0)
-        u_copy(m).start()
+        left = jnp.dot(av[...], pay[dw, :] * inv_tokens, precision=lax.Precision.HIGHEST,
+                       preferred_element_type=jnp.float32)
+        ub[...] = jnp.dot(left, sv[...], precision=lax.Precision.HIGHEST,
+                          preferred_element_type=jnp.float32)
+        for c in u_copies(m):
+            c.start()
+
+        @pl.when(m < 3)
+        def _():
+            for c in inv_copies(m + 1):
+                c.start()
 
     def sym_copy(m):
         return pltpu.make_async_copy(rows_at(pay, base_of(m) * UNIT, 2 * UNIT), sym_out.at[m - 4], osem.at[m - 4])
 
     load(0, 0, 0)
+    for c in inv_copies(0):
+        c.start()
 
     def tick(t, carry):
         for k in range(COPIES, 0, -1):
-            m = t - k
+            m = t - LAG[k]
 
             @pl.when(jnp.logical_and(m >= 0, m < MATS))
             def _(k=k, m=m):
@@ -257,9 +271,6 @@
                 @pl.when(m < 4)
                 def _():
                     stage(k, m, 2)
-                    if k == COPIES - 1:
-                        for c in inv_copies(m):
-                            c.start()
                     if k == COPIES:
                         precondition(m)
 
@@ -288,8 +299,10 @@
 
         return carry
 
-    lax.fori_loop(0, MATS + COPIES, tick, 0)
-    u_copy(3).wait()
+    lax.fori_loop(0, MATS + LAG[COPIES], tick, 0)
+    u_left(3)
+    for m in range(LAYERS):
+        u_copies(m)[1].wait_recv()
 
     def finish(m, carry):
         sym_copy(m).wait()
@@ -313,9 +326,9 @@
             pltpu.VMEM((UNITS * RROWS, D), f32),
             pltpu.VMEM((2, tok // CHUNKS, D), bf16),
             pltpu.VMEM((2, tok // CHUNKS, D), bf16),
+            pltpu.VMEM((HROWS, D), f32),
             pltpu.VMEM((D, D), f32),
-            pltpu.VMEM((D, D), f32),
-            pltpu.VMEM((D, D), f32),
+            pltpu.VMEM((HROWS, D), f32),
             pltpu.SemaphoreType.DMA((MATS, 3, COPIES)),
             pltpu.SemaphoreType.DMA((MATS, 3, COPIES)),
             pltpu.SemaphoreType.REGULAR((MATS, 3, HALVINGS)),
@@ -323,6 +336,8 @@
             pltpu.SemaphoreType.DMA((2,)),
             pltpu.SemaphoreType.DMA((2,)),
             pltpu.SemaphoreType.DMA((1,)),
+            pltpu.SemaphoreType.DMA((LAYERS,)),
+            pltpu.SemaphoreType.DMA((LAYERS,)),
             pltpu.SemaphoreType.DMA((8,)),
         ],
         compiler_params=pltpu.CompilerParams(collective_id=0, has_side_effects=True, vmem_limit_bytes=66 * 1000 * 1000),

time: 330 us -> 308 us (0.933)
  Pallas kernels: 260 us -> 237 us
    pallas_call x1, Pallas kernels: 240 us -> 217 us  [reduce_all(): pl.pallas_call(functools.partial(reduce_kernel, 1.0 / tokens), out_shape=...]
where the time goes in v2:
time: 308 us; the launch traced here: 306 us
  Pallas kernels  237 us (77%)
  matrix products  57.7 us (19%)
  local copies, waits for them, and re-layouts  10.7 us (3%)
    pallas_call x1, Pallas kernels, reduce_all(): pl.pallas_call(functools.partial(reduce_kernel, 1.0 / tokens), out_shape=...  217 us
    dot_general x3, matrix products, local_step(): jnp.dot(acts[-1], w_stack[i], preferred_element_type=jnp.float32)  29.1 us
    dot_general x3, matrix products, times_wt(): lax.dot_general(g_rows, w_mat, (((1,), (1,)), ((), ())), preferred_elemen...  28.6 us
    pallas_call x1, Pallas kernels, fold(): pl.pallas_call(functools.partial(fold_kernel, (1.0 - RHO) / tokens), out_...  19.8 us
    unnamed x17, local copies, waits for them, and re-layouts  10.7 us

profile of v2, /device:TPU:0, one launch (start us, length us, event | category | flops | bytes accessed | tf_op | source)
XLA Modules:
  0.0 306.3 jit_solution(6452282867658138297)
XLA Ops:
  0.6 0.0 copy-start
  0.6 8.3 %fusion.1 = (bf16[4096,768]{1,0:T(8,128)(2,1)S(1)}, bf16[4096,768]{1,0:T(8,128)(2,1)S(1)}) fusion(bf16[4096,768]{1,0:T(8,128)(2,1)} %x.1, bf16[4,768,768]{2,1,0:T(8,128)(2,1)} %param.9), kind=kOutput, calls=%fused_computation.16 | convolution fusion | flops 4853858304 | bytes 20054016 | tf_op jit(solution)/shard_map/dot_general | solution.py:393
  8.9 0.0 copy-start.1
  9.0 0.0 copy-done
  9.0 0.0 slice-start
  9.0 9.8 %fusion.10 = (bf16[4096,768]{1,0:T(8,128)(2,1)}, bf16[4096,768]{1,0:T(8,128)(2,1)}) fusion(bf16[4096,768]{1,0:T(8,128)(2,1)S(1)} %get-tuple-element.11.h1, bf16[4,768,768]{2,1,0:T(8,128)(2,1)S(1)} %copy-done), kind=kOutput, calls=%fused_computation.25 | convolution fusion | flops 4853858304 | bytes 20054016 | tf_op jit(solution)/shard_map/dot_general | solution.py:393
  18.8 0.0 copy-done.1
  18.8 0.0 slice-start.1
  18.8 11.0 %fusion.19 = (bf16[4096,768]{1,0:T(8,128)(2,1)}, bf16[4096,768]{1,0:T(8,128)(2,1)}) fusion(bf16[4096,768]{1,0:T(8,128)(2,1)} %get-tuple-element.13.h2, bf16[4,768,768]{2,1,0:T(8,128)(2,1)S(1)} %copy-done), kind=kOutput, calls=%fused_computation.34 | convolution fusion | flops 4853858304 | bytes 20054016 | tf_op jit(solution)/shard_map/dot_general | solution.py:393
  29.8 0.0 slice-done
  29.8 0.0 slice-done.1
  29.8 0.0 slice-start.3
  29.8 10.1 %fusion.26.g3 = bf16[4096,768]{1,0:T(8,128)(2,1)S(1)} fusion(bf16[4096,768]{1,0:T(8,128)(2,1)} %get-tuple-element.16, bf16[4096,768]{1,0:T(8,128)(2,1)S(1)} %bitcast.35, bf16[4,768,768]{2,1,0:T(8,128)(2,1)S(1)} %copy-done), kind=kOutput, calls=%fused_computation.41 | convolution fusion | flops 4872732672 | bytes 20054016 | tf_op jit(solution)/shard_map/dot_general | solution.py:40
  39.9 0.0 slice-done.2
  39.9 0.0 slice-done.3
  39.9 0.0 copy-start.2
  39.9 8.8 %fusion.17.g2 = bf16[4096,768]{1,0:T(8,128)(2,1)S(1)} fusion(bf16[4096,768]{1,0:T(8,128)(2,1)S(1)} %bitcast.37, bf16[4096,768]{1,0:T(8,128)(2,1)S(1)} %fusion.26.g3, bf16[4,768,768]{2,1,0:T(8,128)(2,1)S(1)} %copy-done), kind=kOutput, calls=%fused_computation.32 | convolution fusion | flops 4872732672 | bytes 20054016 | tf_op jit(solution)/shard_map/dot_general | solution.py:40
  48.7 0.0 copy-done.2
  48.8 0.0 copy-start.3
  48.8 2.6 copy-done.3
  51.4 9.7 %fusion.8.g1 = bf16[4096,768]{1,0:T(8,128)(2,1)} fusion(bf16[4096,768]{1,0:T(8,128)(2,1)S(1)} %get-tuple-element.12, bf16[4096,768]{1,0:T(8,128)(2,1)S(1)} %fusion.17.g2, bf16[4,768,768]{2,1,0:T(8,128)(2,1)S(1)} %copy-done), kind=kOutput, calls=%fused_computation.23 | convolution fusion | flops 4872732672 | bytes 20054016 | tf_op jit(solution)/shard_map/dot_general | solution.py:40
  61.1 217.4 %token_sums_reduced.1 = (f32[8,512,768]{2,1,0:T(8,128)}, f32[4,768,768]{2,1,0:T(8,128)}) custom-call(bf16[4096,768]{1,0:T(8,128)(2,1)} %x.1, bf16[4096,768]{1,0:T(8,128)(2,1)} %copy-done.1, bf16[4096,768]{1,0:T(8,128)(2,1)} %get-tuple-element.13.h2, bf16[4096,768]{1,0:T(8,128)(2,1)} %get-tuple-element.15.h3, bf16[4096,768]{1,0:T(8,128)(2,1)} %fusion.8.g1, ...), custom_call_target="tpu_custom_call" | custom-call | flops 91804925952 | bytes 100663296 | tf_op jit(solution)/shard_map/token_sums_reduced/pallas_call | solution.py:319
  278.5 19.8 %fold_factors.1 = (f32[4,768,768]{2,1,0:T(8,128)}, f32[4,768,768]{2,1,0:T(8,128)}) custom-call(f32[8,512,768]{2,1,0:T(8,128)} %get-tuple-element.8.pa.ps, f32[8,512,768]{2,1,0:T(8,128)} %get-tuple-element.8.pa.ps, f32[4,768,768]{2,1,0:T(8,128)} %ao.1, f32[4,768,768]{2,1,0:T(8,128)} %so.1), custom_call_target="tpu_custom_call" | custom-call | tf_op jit(solution)/shard_map/fold_factors/pallas_call | solution.py:374
  298.3 8.0 %copy.11 = f32[4,768,768]{2,1,0:T(8,128)} copy(f32[4,768,768]{2,1,0:T(8,128)} %get-tuple-element.20) | data formatting | bytes 18874368
  (3 shorter events, 0.0 us)
Async XLA Ops:
  0.6 8.3 %copy-start = (bf16[4,768,768]{2,1,0:T(8,128)(2,1)S(1)}, bf16[4,768,768]{2,1,0:T(8,128)(2,1)}, u32[]{:S(2)}) copy-start(bf16[4,768,768]{2,1,0:T(8,128)(2,1)} %param.9) | copy-start | bytes 14155780
  8.9 9.8 %copy-start.1 = (bf16[4096,768]{1,0:T(8,128)(2,1)}, bf16[4096,768]{1,0:T(8,128)(2,1)S(1)}, u32[]{:S(2)}) copy-start(bf16[4096,768]{1,0:T(8,128)(2,1)S(1)} %get-tuple-element.11.h1) | copy-start | bytes 18874372
  9.0 20.8 %slice-start = ((s8[6291456]{0:T(1024)(128)(4,1)}), s8[4194304]{0:T(1024)(128)(4,1)S(1)}, s32[]{:S(2)}) async-start(s8[6291456]{0:T(1024)(128)(4,1)} %bitcast.34), calls=%async_computation | async-start | bytes 8388608
  18.8 11.0 %slice-start.1 = ((s8[6291456]{0:T(1024)(128)(4,1)}), s8[2097152]{0:T(1024)(128)(4,1)S(1)}, s32[]{:S(2)}) async-start(s8[6291456]{0:T(1024)(128)(4,1)} %bitcast.34), calls=%async_computation.1 | async-start | bytes 4194304
  18.8 21.1 %slice-start.2 = ((s8[6291456]{0:T(1024)(128)(4,1)}), s8[4194304]{0:T(1024)(128)(4,1)S(1)}, s32[]{:S(2)}) async-start(s8[6291456]{0:T(1024)(128)(4,1)} %bitcast.36), calls=%async_computation.2 | async-start | bytes 8388608
  29.8 10.1 %slice-start.3 = ((s8[6291456]{0:T(1024)(128)(4,1)}), s8[2097152]{0:T(1024)(128)(4,1)S(1)}, s32[]{:S(2)}) async-start(s8[6291456]{0:T(1024)(128)(4,1)} %bitcast.36), calls=%async_computation.3 | async-start | bytes 4194304
  39.9 8.8 %copy-start.2 = (bf16[4096,768]{1,0:T(8,128)(2,1)}, bf16[4096,768]{1,0:T(8,128)(2,1)S(1)}, u32[]{:S(2)}) copy-start(bf16[4096,768]{1,0:T(8,128)(2,1)S(1)} %fusion.26.g3) | copy-start | bytes 18874372
  48.8 2.6 copy-start.3

commit v3 on v2

--- a/solution.py
+++ b/solution.py
@@ -17,6 +17,7 @@
 UNIT = 256
 HROWS = 384
 MATS = 12
+BLOCKS = 16
 UNITS = 28
 HALVINGS = 4
 COPIES = 2 * HALVINGS + 1
@@ -24,7 +25,8 @@
 MESH = pl.DeviceIdType.MESH
 ORDERS = ((1, 2, 4, 8, 16), (1, 4, 2, 8, 16), (1, 8, 16, 2, 4))
 CHUNKS = 4
-LAG = (0, 1, 3, 5, 7, 9, 11, 13, 15, 16)
+ENTER = 18
+PUMPS = ENTER + COPIES
 DN0 = (((0,), (0,)), ((), ()))
 
 
@@ -48,15 +50,19 @@
     return 256 - (256 >> step)
 
 
-def reduce_kernel(inv_tokens, x, h1, h2, h3, g1, g2, g3, dy, ainv, sinv,
-                  sym_out, u_out,
-                  pay, rbuf, lbuf, gbuf, av, sv, ub,
+def reduce_kernel(inv_tokens, x, dy, w, ainv, sinv,
+                  sym_out, u_out, hs, zs, gs,
+                  pay, rbuf, lbuf, gbuf, av, sv, ub, wb, cin, cz, cout,
+                  wsem, cisem, czsem, cosem,
                   ssem, rsem, fsem, lsem, gsem, isem, usem, ussem, ursem, osem):
     me = lax.axis_index("data")
     tok = x.shape[0]
     chunk = tok // CHUNKS
-    acts = (x, h1, h2, h3)
-    grads = (g1, g2, g3, dy)
+    acts = (x, hs.at[0], hs.at[1], hs.at[2])
+    grads = (gs.at[0], gs.at[1], gs.at[2], dy)
+    operands = ((dy, None), (x, None), (acts[1], None), (acts[2], None),
+                (acts[3], dy), (acts[2], grads[2]), (acts[1], grads[1]), (x, grads[0]),
+                (acts[3], None), (grads[2], None), (grads[1], None), (grads[0], None))
 
     def bit(mask):
         return lax.rem(lax.div(me, mask), 2)
@@ -76,8 +82,7 @@
         return off
 
     def base_of(m):
-        late = lax.div(m + 8, 12)
-        return 3 * m - late * (m - 4)
+        return 2 * m + lax.div(m + 8, 12) * (m - 4) - lax.div(m + 4, 12) * (m - 8)
 
     def rows_at(ref, start, size):
         return ref.at[pl.ds(pl.multiple_of(start, 8), size), :]
@@ -168,10 +173,7 @@
     def load(m, kc, slot):
         rows = pl.ds(kc * chunk, chunk)
         for i in range(MATS):
-            if i < 4:
-                left, right = acts[3 - i], grads[3 - i]
-            else:
-                left, right = (acts + grads)[i - 4], None
+            left, right = operands[i]
 
             @pl.when(m == i)
             def _(left=left, right=right):
@@ -239,7 +241,7 @@
         def _():
             u_left(m - 1)
 
-        dw = pl.ds(pl.multiple_of(3 * m * UNIT, 8), D)
+        dw = pl.ds(pl.multiple_of((8 + 3 * m) * UNIT, 8), D)
         left = jnp.dot(av[...], pay[dw, :] * inv_tokens, precision=lax.Precision.HIGHEST,
                        preferred_element_type=jnp.float32)
         ub[...] = jnp.dot(left, sv[...], precision=lax.Precision.HIGHEST,
@@ -253,74 +255,200 @@
                 c.start()
 
     def sym_copy(m):
-        return pltpu.make_async_copy(rows_at(pay, base_of(m) * UNIT, 2 * UNIT), sym_out.at[m - 4], osem.at[m - 4])
-
+        place = m - 4 * lax.div(m + 4, 12)
+        return pltpu.make_async_copy(rows_at(pay, base_of(m) * UNIT, 2 * UNIT), sym_out.at[place], osem.at[place])
+
+    block = tok // BLOCKS
+
+    def block_rows(b):
+        return pl.ds(pl.multiple_of(b * block, 8), block)
+
+    def w_copy(step):
+        layer = step + lax.div(step, 3) * (6 - 2 * step)
+        return pltpu.make_async_copy(w.at[layer], wb.at[lax.rem(step, 2)], wsem.at[lax.rem(step, 2)])
+
+    def w_next(step):
+        w_copy(step).wait()
+
+        @pl.when(step < 5)
+        def _():
+            w_copy(step + 1).start()
+
+    def first_in(first, other, is_first, b, slot):
+        @pl.when(is_first)
+        def _():
+            pltpu.make_async_copy(first.at[block_rows(b), :], cin.at[slot], cisem.at[slot]).start()
+
+        @pl.when(jnp.logical_not(is_first))
+        def _():
+            pltpu.make_async_copy(other.at[block_rows(b), :], cin.at[slot], cisem.at[slot]).start()
+
+    def z_in(i, b, slot):
+        return pltpu.make_async_copy(zs.at[i, block_rows(b), :], cz.at[slot], czsem.at[slot])
+
+    def z_out(i, b, slot):
+        return pltpu.make_async_copy(cz.at[slot], zs.at[i, block_rows(b), :], czsem.at[slot])
+
+    def out_copy(dst, b, slot):
+        return pltpu.make_async_copy(cout.at[slot], dst.at[block_rows(b), :], cosem.at[slot])
+
+    def forward(i):
+        prev = hs.at[lax.rem(i + 2, 3)]
+        dst = hs.at[i]
+        w_next(i)
+        weight = lax.rem(i, 2)
+        first_in(x, prev, i == 0, 0, 0)
+
+        def one(b, carry):
+            slot = lax.rem(b, 2)
+
+            @pl.when(b + 1 < BLOCKS)
+            def _():
+                first_in(x, prev, i == 0, b + 1, 1 - slot)
+
+            pltpu.make_async_copy(x.at[block_rows(b), :], cin.at[slot], cisem.at[slot]).wait()
+
+            @pl.when(b >= 2)
+            def _():
+                z_out(i, b - 2, slot).wait()
+                out_copy(dst, b - 2, slot).wait()
+
+            z_val = jnp.dot(cin[slot], wb[weight], preferred_element_type=jnp.float32).astype(jnp.bfloat16)
+            cz[slot] = z_val
+            cout[slot] = gelu_fwd(z_val.astype(jnp.float32)).astype(jnp.bfloat16)
+            z_out(i, b, slot).start()
+            out_copy(dst, b, slot).start()
+            return carry
+
+        lax.fori_loop(0, BLOCKS, one, 0)
+        for b in (BLOCKS - 2, BLOCKS - 1):
+            z_out(i, b, b % 2).wait()
+            out_copy(dst, b, b % 2).wait()
+
+    def backward(i):
+        prev = gs.at[lax.rem(i + 1, 3)]
+        dst = gs.at[i]
+        step = 5 - i
+        w_next(step)
+        weight = lax.rem(step, 2)
+        first_in(dy, prev, i == 2, 0, 0)
+        z_in(i, 0, 0).start()
+
+        def one(b, carry):
+            slot = lax.rem(b, 2)
+
+            @pl.when(b + 1 < BLOCKS)
+            def _():
+                first_in(dy, prev, i == 2, b + 1, 1 - slot)
+                z_in(i, b + 1, 1 - slot).start()
+
+            pltpu.make_async_copy(dy.at[block_rows(b), :], cin.at[slot], cisem.at[slot]).wait()
+            z_in(i, b, slot).wait()
+
+            @pl.when(b >= 2)
+            def _():
+                out_copy(dst, b - 2, slot).wait()
+
+            dh = times_wt(cin[slot], wb[weight]).astype(jnp.bfloat16)
+            cout[slot] = (dh.astype(jnp.float32) * gelu_slope(cz[slot].astype(jnp.float32))).astype(jnp.bfloat16)
+            out_copy(dst, b, slot).start()
+            return carry
+
+        lax.fori_loop(0, BLOCKS, one, 0)
+        for b in (BLOCKS - 2, BLOCKS - 1):
+            out_copy(dst, b, b % 2).wait()
+
+    def enters(e):
+        return jnp.logical_and(jnp.logical_and(e >= 0, e < ENTER), jnp.logical_or(e >= 12, lax.rem(e, 2) == 0))
+
+    def matrix(e):
+        late = lax.div(e, 12)
+        return (1 - late) * lax.div(e, 2) + late * (e - 6)
+
+    def is_dw(m):
+        return jnp.logical_and(m >= 4, m < 8)
+
+    w_copy(0).start()
     load(0, 0, 0)
     for c in inv_copies(0):
         c.start()
 
-    def tick(t, carry):
-        for k in range(COPIES, 0, -1):
-            m = t - LAG[k]
-
-            @pl.when(jnp.logical_and(m >= 0, m < MATS))
-            def _(k=k, m=m):
+    def pump(q, carry):
+        for k in range(1, COPIES + 1):
+            e = q - k
+
+            @pl.when(enters(e))
+            def _(k=k, e=e):
+                m = matrix(e)
                 stage(k, m, 0)
                 stage(k, m, 1)
 
-                @pl.when(m < 4)
+                @pl.when(is_dw(m))
                 def _():
                     stage(k, m, 2)
                     if k == COPIES:
-                        precondition(m)
+                        precondition(m - 4)
 
                 if k == COPIES:
-                    @pl.when(m >= 4)
+                    @pl.when(jnp.logical_not(is_dw(m)))
                     def _():
                         sym_copy(m).start()
 
-        @pl.when(t < MATS)
-        def _():
-            @pl.when(t < 4)
-            def _():
-                gram_dw(t)
-
-            @pl.when(t >= 4)
-            def _():
-                gram_sym(t)
-
-            load(t + 1, 0, 0)
-            scatter_copy(t, 0, 0).start()
-            scatter_copy(t, 1, 0).start()
-
-            @pl.when(t < 4)
-            def _():
-                scatter_copy(t, 2, 0).start()
+        @pl.when(enters(q))
+        def _():
+            m = matrix(q)
+
+            @pl.when(is_dw(m))
+            def _():
+                gram_dw(m)
+
+            @pl.when(jnp.logical_not(is_dw(m)))
+            def _():
+                gram_sym(m)
+
+            load(m + 1, 0, 0)
+            scatter_copy(m, 0, 0).start()
+            scatter_copy(m, 1, 0).start()
+
+            @pl.when(is_dw(m))
+            def _():
+                scatter_copy(m, 2, 0).start()
+
+        @pl.when(jnp.logical_and(q < 12, lax.rem(q, 2) == 1))
+        def _():
+            step = lax.div(q, 2)
+
+            @pl.when(step < 3)
+            def _():
+                forward(step)
+
+            @pl.when(step >= 3)
+            def _():
+                backward(5 - step)
 
         return carry
 
-    lax.fori_loop(0, MATS + LAG[COPIES], tick, 0)
+    lax.fori_loop(0, PUMPS, pump, 0)
     u_left(3)
     for m in range(LAYERS):
         u_copies(m)[1].wait_recv()
 
-    def finish(m, carry):
+    for m in (0, 1, 2, 3, 8, 9, 10, 11):
         sym_copy(m).wait()
-        return carry
-
-    lax.fori_loop(4, MATS, finish, 0)
-
-
-def reduce_all(arrays, ainv, sinv, tokens):
+
+
+def reduce_all(x, dy, w, ainv, sinv, tokens):
     any_spec = pl.BlockSpec(memory_space=pl.ANY)
-    tok = arrays[0].shape[0]
+    tok = x.shape[0]
     f32, bf16 = jnp.float32, jnp.bfloat16
-    flops = 2 * tok * D * D * 10 + 8 * 12 * D ** 3
-    return pl.pallas_call(
+    flops = 2 * tok * D * D * 16 + 8 * 12 * D ** 3
+    saved = jax.ShapeDtypeStruct((LAYERS - 1, tok, D), bf16)
+    outs = pl.pallas_call(
         functools.partial(reduce_kernel, 1.0 / tokens),
-        out_shape=(jax.ShapeDtypeStruct((8, 2 * UNIT, D), f32), jax.ShapeDtypeStruct((LAYERS, D, D), f32)),
-        in_specs=[any_spec] * 10,
-        out_specs=(any_spec, any_spec),
+        out_shape=(jax.ShapeDtypeStruct((8, 2 * UNIT, D), f32), jax.ShapeDtypeStruct((LAYERS, D, D), f32),
+                   saved, saved, saved),
+        in_specs=[any_spec] * 5,
+        out_specs=(any_spec,) * 5,
         scratch_shapes=[
             pltpu.VMEM((UNITS * UNIT, D), f32),
             pltpu.VMEM((UNITS * RROWS, D), f32),
@@ -329,6 +457,14 @@
             pltpu.VMEM((HROWS, D), f32),
             pltpu.VMEM((D, D), f32),
             pltpu.VMEM((HROWS, D), f32),
+            pltpu.VMEM((2, D, D), bf16),
+            pltpu.VMEM((2, tok // BLOCKS, D), bf16),
+            pltpu.VMEM((2, tok // BLOCKS, D), bf16),
+            pltpu.VMEM((2, tok // BLOCKS, D), bf16),
+            pltpu.SemaphoreType.DMA((2,)),
+            pltpu.SemaphoreType.DMA((2,)),
+            pltpu.SemaphoreType.DMA((2,)),
+            pltpu.SemaphoreType.DMA((2,)),
             pltpu.SemaphoreType.DMA((MATS, 3, COPIES)),
             pltpu.SemaphoreType.DMA((MATS, 3, COPIES)),
             pltpu.SemaphoreType.REGULAR((MATS, 3, HALVINGS)),
@@ -340,14 +476,16 @@
             pltpu.SemaphoreType.DMA((LAYERS,)),
             pltpu.SemaphoreType.DMA((8,)),
         ],
-        compiler_params=pltpu.CompilerParams(collective_id=0, has_side_effects=True, vmem_limit_bytes=66 * 1000 * 1000),
-        cost_estimate=pl.CostEstimate(flops=flops, bytes_accessed=8 * tok * D * 4, transcendentals=0),
+        compiler_params=pltpu.CompilerParams(collective_id=0, has_side_effects=True, vmem_limit_bytes=67 * 1000 * 1000),
+        cost_estimate=pl.CostEstimate(flops=flops, bytes_accessed=16 * tok * D * 4, transcendentals=0),
         name="token_sums_reduced",
-    )(*arrays, ainv, sinv)
-
-
-def fold_kernel(scale, pa, ps, ao, so, an, sn):
+    )(x, dy, w, ainv, sinv)
+    return outs[0], outs[1]
+
+
+def fold_kernel(scale, pa, ps, ao, so, u_in, an, sn, u_out):
     strip = pl.program_id(1)
+    u_out[...] = u_in[...]
     for packed, old, new in ((pa, ao, an), (ps, so, sn)):
         @pl.when(strip == 0)
         def _(packed=packed, old=old, new=new):
@@ -365,41 +503,29 @@
             new[0, :, 2 * BLK:] = RHO * old[0, :, 2 * BLK:] + scale * packed[0, BLK:, 2 * BLK:]
 
 
-def fold(packed, a_old, s_old, tokens):
+def fold(packed, a_old, s_old, u_stack, tokens):
     f32 = jnp.float32
-    pack_a = pl.BlockSpec((1, 2 * UNIT, D), lambda l, i: (l, 0, 0))
-    pack_s = pl.BlockSpec((1, 2 * UNIT, D), lambda l, i: (l + LAYERS, 0, 0))
+    pack_a = pl.BlockSpec((1, 2 * UNIT, D), lambda l, i: (l + 1, 0, 0))
+    pack_s = pl.BlockSpec((1, 2 * UNIT, D), lambda l, i: ((7 - l) * (1 - l // 3), 0, 0))
     strip = pl.BlockSpec((1, BLK, D), lambda l, i: (l, i, 0))
     shape = jax.ShapeDtypeStruct((LAYERS, D, D), f32)
     return pl.pallas_call(
         functools.partial(fold_kernel, (1.0 - RHO) / tokens),
-        out_shape=(shape, shape),
+        out_shape=(shape, shape, shape),
         grid=(LAYERS, 3),
-        in_specs=[pack_a, pack_s, strip, strip],
-        out_specs=(strip, strip),
+        in_specs=[pack_a, pack_s, strip, strip, strip],
+        out_specs=(strip, strip, strip),
         name="fold_factors",
-    )(packed, packed, a_old, s_old)
+    )(packed, packed, a_old, s_old, u_stack)
 
 
 def solution(mesh):
     group_size = mesh.shape["data"]
 
     def local_step(x_loc, dy_loc, w_stack, a_old, s_old, a_inv, s_inv):
-        layers = w_stack.shape[0]
         tokens = x_loc.shape[0] * group_size
-        acts = [x_loc]
-        pre = []
-        for i in range(layers - 1):
-            z = jnp.dot(acts[-1], w_stack[i], preferred_element_type=jnp.float32).astype(jnp.bfloat16)
-            pre.append(z)
-            acts.append(gelu_fwd(z.astype(jnp.float32)).astype(jnp.bfloat16))
-        grads = [None] * layers
-        grads[-1] = dy_loc
-        for i in reversed(range(layers - 1)):
-            dh = times_wt(grads[i + 1], w_stack[i + 1]).astype(jnp.bfloat16)
-            grads[i] = (dh.astype(jnp.float32) * gelu_slope(pre[i].astype(jnp.float32))).astype(jnp.bfloat16)
-        packed, u_stack = reduce_all(acts + grads, a_inv, s_inv, tokens)
-        a_new, s_new = fold(packed, a_old, s_old, tokens)
+        packed, u_stack = reduce_all(x_loc, dy_loc, w_stack, a_inv, s_inv, tokens)
+        a_new, s_new, u_stack = fold(packed, a_old, s_old, u_stack, tokens)
         return u_stack, a_new, s_new
 
     row_spec = P("data", None)

time: 308 us -> 336 us (1.091)
  Pallas kernels: 237 us -> 332 us
  matrix products: 57.7 us -> 0 us
  local copies, waits for them, and re-layouts: 10.7 us -> 0 us
    pallas_call x1, Pallas kernels: 217 us -> 307 us  [reduce_all(): pl.pallas_call(functools.partial(reduce_kernel, 1.0 / tokens), out_shape=...]
    dot_general x6 -> x0, matrix products: 57.7 us -> none  [the longest x3 29.1 us: local_step(): jnp.dot(acts[-1], w_stack[i], preferred_element_type=jnp.float32)]
    unnamed x17 -> x0, local copies, waits for them, and re-layouts: 10.7 us -> none
    pallas_call x1, Pallas kernels: 19.8 us -> 24.8 us  [fold(): pl.pallas_call(functools.partial(fold_kernel, (1.0 - RHO) / tokens), out_...]
where the time goes in v3:
time: 336 us; the launch traced here: 332 us
  Pallas kernels  332 us (99%)
    pallas_call x1, Pallas kernels, reduce_all(): pl.pallas_call(functools.partial(reduce_kernel, 1.0 / tokens), out_shape=...  307 us
    pallas_call x1, Pallas kernels, fold(): pl.pallas_call(functools.partial(fold_kernel, (1.0 - RHO) / tokens), out_...  24.8 us

profile of v3, /device:TPU:0, one launch (start us, length us, event | category | flops | bytes accessed | tf_op | source)
XLA Modules:
  0.0 332.4 jit_solution(13143738026091666201)
XLA Ops:
  0.6 307.0 %token_sums_reduced.1 = (f32[8,512,768]{2,1,0:T(8,128)}, f32[4,768,768]{2,1,0:T(8,128)}, bf16[3,4096,768]{2,1,0:T(8,128)(2,1)}, bf16[3,4096,768]{2,1,0:T(8,128)(2,1)}, bf16[3,4096,768]{2,1,0:T(8,128)(2,1)}) custom-call(bf16[4096,768]{1,0:T(8,128)(2,1)} %x.1, bf16[4096,768]{1,0:T(8,128)(2,1)} %dy.1, bf16[4,768,768]{2,1,0:T(8,128)(2,1)} %w.1, ...), custom_call_target="tpu_custom_call" | custom-call | flops 120795955200 | bytes 201326592 | tf_op jit(solution)/shard_map/token_sums_reduced/pallas_call | solution.py:446
  307.6 24.8 %fold_factors.1 = (f32[4,768,768]{2,1,0:T(8,128)}, f32[4,768,768]{2,1,0:T(8,128)}, f32[4,768,768]{2,1,0:T(8,128)}) custom-call(f32[8,512,768]{2,1,0:T(8,128)} %get-tuple-element.8.pa.ps, f32[8,512,768]{2,1,0:T(8,128)} %get-tuple-element.8.pa.ps, f32[4,768,768]{2,1,0:T(8,128)} %ao.1, f32[4,768,768]{2,1,0:T(8,128)} %so.1, f32[4,768,768]{2,1,0:T(8,128)} %get-tuple-element.9.u_in), custom_call_target="tpu_custom_call" | custom-call | tf_op jit(solution)/shard_map/fold_factors/pallas_call | solution.py:512

commit v4 on v3

--- a/solution.py
+++ b/solution.py
@@ -24,7 +24,8 @@
 RROWS = 256
 MESH = pl.DeviceIdType.MESH
 ORDERS = ((1, 2, 4, 8, 16), (1, 4, 2, 8, 16), (1, 8, 16, 2, 4))
-CHUNKS = 4
+CHUNKS = 8
+DEEP = 4
 ENTER = 18
 PUMPS = ENTER + COPIES
 DN0 = (((0,), (0,)), ((), ()))
@@ -164,14 +165,15 @@
             if step > 0:
                 gather_start(m, j, step - 1)
 
-    def wait_left(kc, slot):
-        pltpu.make_async_copy(x.at[pl.ds(kc * chunk, chunk), :], lbuf.at[slot], lsem.at[slot]).wait()
-
-    def wait_right(kc, slot):
-        pltpu.make_async_copy(dy.at[pl.ds(kc * chunk, chunk), :], gbuf.at[slot], gsem.at[slot]).wait()
-
-    def load(m, kc, slot):
-        rows = pl.ds(kc * chunk, chunk)
+    def wait_left(slot):
+        pltpu.make_async_copy(x.at[pl.ds(0, chunk), :], lbuf.at[slot], lsem.at[slot]).wait()
+
+    def wait_right(slot):
+        pltpu.make_async_copy(dy.at[pl.ds(0, chunk), :], gbuf.at[slot], gsem.at[slot]).wait()
+
+    def load(m, kc):
+        rows = pl.ds(pl.multiple_of(kc * chunk, 8), chunk)
+        slot = lax.rem(kc, DEEP)
         for i in range(MATS):
             left, right = operands[i]
 
@@ -188,31 +190,41 @@
         else:
             pay[a, c0:c0 + cols] = pay[a, c0:c0 + cols] + val
 
-    def gram_dw(m):
+    def gram(m, paired):
         row = base_of(m) * UNIT
-        for kc in range(CHUNKS):
-            slot = kc % 2
-            wait_left(kc, slot)
-            wait_right(kc, slot)
-            if kc + 1 < CHUNKS:
-                load(m, kc + 1, 1 - slot)
-            for j in range(3):
-                val = lax.dot_general(lbuf[slot, :, j * BLK:(j + 1) * BLK], gbuf[slot], DN0,
-                                      preferred_element_type=jnp.float32)
-                put(kc == 0, row + j * UNIT, UNIT, 0, D, val)
-
-    def gram_sym(m):
-        row = base_of(m) * UNIT
-        for kc in range(CHUNKS):
-            slot = kc % 2
-            wait_left(kc, slot)
-            if kc + 1 < CHUNKS:
-                load(m, kc + 1, 1 - slot)
-            for j, (unit, c0) in enumerate(((0, 0), (1, 0), (1, 2 * BLK))):
-                cols = D - j * BLK
-                val = lax.dot_general(lbuf[slot, :, j * BLK:(j + 1) * BLK], lbuf[slot, :, j * BLK:], DN0,
-                                      preferred_element_type=jnp.float32)
-                put(kc == 0, row + unit * UNIT, UNIT, c0, cols, val)
+
+        def piece(kc, first):
+            slot = lax.rem(kc, DEEP)
+            wait_left(slot)
+            if paired:
+                wait_right(slot)
+
+            @pl.when(kc + DEEP - 1 < CHUNKS)
+            def _():
+                load(m, kc + DEEP - 1)
+
+            if paired:
+                for j in range(3):
+                    val = lax.dot_general(lbuf[slot, :, j * BLK:(j + 1) * BLK], gbuf[slot], DN0,
+                                          preferred_element_type=jnp.float32)
+                    put(first, row + j * UNIT, UNIT, 0, D, val)
+            else:
+                for j, (unit, c0) in enumerate(((0, 0), (1, 0), (1, 2 * BLK))):
+                    cols = D - j * BLK
+                    val = lax.dot_general(lbuf[slot, :, j * BLK:(j + 1) * BLK], lbuf[slot, :, j * BLK:], DN0,
+                                          preferred_element_type=jnp.float32)
+                    put(first, row + unit * UNIT, UNIT, c0, cols, val)
+
+        def rest(kc, carry):
+            piece(kc, False)
+            return carry
+
+        piece(0, True)
+        lax.fori_loop(1, CHUNKS, rest, 0)
+
+    def load_first(m):
+        for kc in range(DEEP - 1):
+            load(m, kc)
 
     own = pl.ds(pl.multiple_of(bit(1) * HROWS, 8), HROWS)
 
@@ -242,10 +254,12 @@
             u_left(m - 1)
 
         dw = pl.ds(pl.multiple_of((8 + 3 * m) * UNIT, 8), D)
-        left = jnp.dot(av[...], pay[dw, :] * inv_tokens, precision=lax.Precision.HIGHEST,
-                       preferred_element_type=jnp.float32)
-        ub[...] = jnp.dot(left, sv[...], precision=lax.Precision.HIGHEST,
-                          preferred_element_type=jnp.float32)
+        for r in (0, HROWS // 2):
+            a = slice(r, r + HROWS // 2)
+            left = inv_tokens * jnp.dot(av[a, :], pay[dw, :], precision=lax.Precision.HIGHEST,
+                                        preferred_element_type=jnp.float32)
+            ub[a, :] = jnp.dot(left, sv[...], precision=lax.Precision.HIGHEST,
+                               preferred_element_type=jnp.float32)
         for c in u_copies(m):
             c.start()
 
@@ -291,27 +305,31 @@
 
     def out_copy(dst, b, slot):
         return pltpu.make_async_copy(cout.at[slot], dst.at[block_rows(b), :], cosem.at[slot])
+
+    def forward_first(i):
+        prev = hs.at[lax.rem(i + 2, 3)]
+        for b in range(DEEP - 1):
+            first_in(x, prev, i == 0, b, b)
 
     def forward(i):
         prev = hs.at[lax.rem(i + 2, 3)]
         dst = hs.at[i]
         w_next(i)
         weight = lax.rem(i, 2)
-        first_in(x, prev, i == 0, 0, 0)
 
         def one(b, carry):
-            slot = lax.rem(b, 2)
-
-            @pl.when(b + 1 < BLOCKS)
-            def _():
-                first_in(x, prev, i == 0, b + 1, 1 - slot)
+            slot = lax.rem(b, DEEP)
+
+            @pl.when(b + DEEP - 1 < BLOCKS)
+            def _():
+                first_in(x, prev, i == 0, b + DEEP - 1, lax.rem(b + DEEP - 1, DEEP))
 
             pltpu.make_async_copy(x.at[block_rows(b), :], cin.at[slot], cisem.at[slot]).wait()
 
-            @pl.when(b >= 2)
-            def _():
-                z_out(i, b - 2, slot).wait()
-                out_copy(dst, b - 2, slot).wait()
+            @pl.when(b >= DEEP)
+            def _():
+                z_out(i, b - DEEP, slot).wait()
+                out_copy(dst, b - DEEP, slot).wait()
 
             z_val = jnp.dot(cin[slot], wb[weight], preferred_element_type=jnp.float32).astype(jnp.bfloat16)
             cz[slot] = z_val
@@ -321,9 +339,15 @@
             return carry
 
         lax.fori_loop(0, BLOCKS, one, 0)
-        for b in (BLOCKS - 2, BLOCKS - 1):
-            z_out(i, b, b % 2).wait()
-            out_copy(dst, b, b % 2).wait()
+        for b in range(BLOCKS - DEEP, BLOCKS):
+            z_out(i, b, b % DEEP).wait()
+            out_copy(dst, b, b % DEEP).wait()
+
+    def backward_first(i):
+        prev = gs.at[lax.rem(i + 1, 3)]
+        for b in range(DEEP - 1):
+            first_in(dy, prev, i == 2, b, b)
+            z_in(i, b, b).start()
 
     def backward(i):
         prev = gs.at[lax.rem(i + 1, 3)]
@@ -331,23 +355,22 @@
         step = 5 - i
         w_next(step)
         weight = lax.rem(step, 2)
-        first_in(dy, prev, i == 2, 0, 0)
-        z_in(i, 0, 0).start()
 
         def one(b, carry):
-            slot = lax.rem(b, 2)
-
-            @pl.when(b + 1 < BLOCKS)
-            def _():
-                first_in(dy, prev, i == 2, b + 1, 1 - slot)
-                z_in(i, b + 1, 1 - slot).start()
+            slot = lax.rem(b, DEEP)
+
+            @pl.when(b + DEEP - 1 < BLOCKS)
+            def _():
+                ahead = lax.rem(b + DEEP - 1, DEEP)
+                first_in(dy, prev, i == 2, b + DEEP - 1, ahead)
+                z_in(i, b + DEEP - 1, ahead).start()
 
             pltpu.make_async_copy(dy.at[block_rows(b), :], cin.at[slot], cisem.at[slot]).wait()
             z_in(i, b, slot).wait()
 
-            @pl.when(b >= 2)
-            def _():
-                out_copy(dst, b - 2, slot).wait()
+            @pl.when(b >= DEEP)
+            def _():
+                out_copy(dst, b - DEEP, slot).wait()
 
             dh = times_wt(cin[slot], wb[weight]).astype(jnp.bfloat16)
             cout[slot] = (dh.astype(jnp.float32) * gelu_slope(cz[slot].astype(jnp.float32))).astype(jnp.bfloat16)
@@ -355,8 +378,8 @@
             return carry
 
         lax.fori_loop(0, BLOCKS, one, 0)
-        for b in (BLOCKS - 2, BLOCKS - 1):
-            out_copy(dst, b, b % 2).wait()
+        for b in range(BLOCKS - DEEP, BLOCKS):
+            out_copy(dst, b, b % DEEP).wait()
 
     def enters(e):
         return jnp.logical_and(jnp.logical_and(e >= 0, e < ENTER), jnp.logical_or(e >= 12, lax.rem(e, 2) == 0))
@@ -369,11 +392,22 @@
         return jnp.logical_and(m >= 4, m < 8)
 
     w_copy(0).start()
-    load(0, 0, 0)
+    load_first(0)
     for c in inv_copies(0):
         c.start()
 
     def pump(q, carry):
+        chained = jnp.logical_and(q < 12, lax.rem(q, 2) == 1)
+        step = lax.div(q, 2)
+
+        @pl.when(jnp.logical_and(chained, step < 3))
+        def _():
+            forward_first(step)
+
+        @pl.when(jnp.logical_and(chained, step >= 3))
+        def _():
+            backward_first(5 - step)
+
         for k in range(1, COPIES + 1):
             e = q - k
 
@@ -400,13 +434,13 @@
 
             @pl.when(is_dw(m))
             def _():
-                gram_dw(m)
+                gram(m, True)
 
             @pl.when(jnp.logical_not(is_dw(m)))
             def _():
-                gram_sym(m)
-
-            load(m + 1, 0, 0)
+                gram(m, False)
+
+            load_first(m + 1)
             scatter_copy(m, 0, 0).start()
             scatter_copy(m, 1, 0).start()
 
@@ -414,17 +448,13 @@
             def _():
                 scatter_copy(m, 2, 0).start()
 
-        @pl.when(jnp.logical_and(q < 12, lax.rem(q, 2) == 1))
-        def _():
-            step = lax.div(q, 2)
-
-            @pl.when(step < 3)
-            def _():
-                forward(step)
-
-            @pl.when(step >= 3)
-            def _():
-                backward(5 - step)
+        @pl.when(jnp.logical_and(chained, step < 3))
+        def _():
+            forward(step)
+
+        @pl.when(jnp.logical_and(chained, step >= 3))
+        def _():
+            backward(5 - step)
 
         return carry
 
@@ -452,24 +482,24 @@
         scratch_shapes=[
             pltpu.VMEM((UNITS * UNIT, D), f32),
             pltpu.VMEM((UNITS * RROWS, D), f32),
-            pltpu.VMEM((2, tok // CHUNKS, D), bf16),
-            pltpu.VMEM((2, tok // CHUNKS, D), bf16),
+            pltpu.VMEM((DEEP, tok // CHUNKS, D), bf16),
+            pltpu.VMEM((DEEP, tok // CHUNKS, D), bf16),
             pltpu.VMEM((HROWS, D), f32),
             pltpu.VMEM((D, D), f32),
             pltpu.VMEM((HROWS, D), f32),
             pltpu.VMEM((2, D, D), bf16),
-            pltpu.VMEM((2, tok // BLOCKS, D), bf16),
-            pltpu.VMEM((2, tok // BLOCKS, D), bf16),
-            pltpu.VMEM((2, tok // BLOCKS, D), bf16),
+            pltpu.VMEM((DEEP, tok // BLOCKS, D), bf16),
+            pltpu.VMEM((DEEP, tok // BLOCKS, D), bf16),
+            pltpu.VMEM((DEEP, tok // BLOCKS, D), bf16),
             pltpu.SemaphoreType.DMA((2,)),
-            pltpu.SemaphoreType.DMA((2,)),
-            pltpu.SemaphoreType.DMA((2,)),
-            pltpu.SemaphoreType.DMA((2,)),
+            pltpu.SemaphoreType.DMA((DEEP,)),
+            pltpu.SemaphoreType.DMA((DEEP,)),
+            pltpu.SemaphoreType.DMA((DEEP,)),
             pltpu.SemaphoreType.DMA((MATS, 3, COPIES)),
             pltpu.SemaphoreType.DMA((MATS, 3, COPIES)),
             pltpu.SemaphoreType.REGULAR((MATS, 3, HALVINGS)),
-            pltpu.SemaphoreType.DMA((2,)),
-            pltpu.SemaphoreType.DMA((2,)),
+            pltpu.SemaphoreType.DMA((DEEP,)),
+            pltpu.SemaphoreType.DMA((DEEP,)),
             pltpu.SemaphoreType.DMA((2,)),
             pltpu.SemaphoreType.DMA((1,)),
             pltpu.SemaphoreType.DMA((LAYERS,)),

time: 336 us -> 289 us (0.86); the launches traced: 332 us -> 289 us
  Pallas kernels: 332 us -> 288 us
    pallas_call x1, Pallas kernels: 307 us -> 264 us  [reduce_all(): pl.pallas_call(functools.partial(reduce_kernel, 1.0 / tokens), out_shape=...]
where the time goes in v4:
time: 289 us
  Pallas kernels  288 us (100%)
    pallas_call x1, Pallas kernels, reduce_all(): pl.pallas_call(functools.partial(reduce_kernel, 1.0 / tokens), out_shape=...  264 us
    pallas_call x1, Pallas kernels, fold(): pl.pallas_call(functools.partial(fold_kernel, (1.0 - RHO) / tokens), out_...  24.8 us

profile of v4, /device:TPU:0, one launch (start us, length us, event | category | flops | bytes accessed | tf_op | source)
XLA Modules:
  0.0 289.0 jit_solution(13346509562877327935)
XLA Ops:
  0.6 263.5 %token_sums_reduced.1 = (f32[8,512,768]{2,1,0:T(8,128)}, f32[4,768,768]{2,1,0:T(8,128)}, bf16[3,4096,768]{2,1,0:T(8,128)(2,1)}, bf16[3,4096,768]{2,1,0:T(8,128)(2,1)}, bf16[3,4096,768]{2,1,0:T(8,128)(2,1)}) custom-call(bf16[4096,768]{1,0:T(8,128)(2,1)} %x.1, bf16[4096,768]{1,0:T(8,128)(2,1)} %dy.1, bf16[4,768,768]{2,1,0:T(8,128)(2,1)} %w.1, ...), custom_call_target="tpu_custom_call" | custom-call | flops 120795955200 | bytes 201326592 | tf_op jit(solution)/shard_map/token_sums_reduced/pallas_call | solution.py:476
  264.1 24.8 %fold_factors.1 = (f32[4,768,768]{2,1,0:T(8,128)}, f32[4,768,768]{2,1,0:T(8,128)}, f32[4,768,768]{2,1,0:T(8,128)}) custom-call(f32[8,512,768]{2,1,0:T(8,128)} %get-tuple-element.8.pa.ps, f32[8,512,768]{2,1,0:T(8,128)} %get-tuple-element.8.pa.ps, f32[4,768,768]{2,1,0:T(8,128)} %ao.1, f32[4,768,768]{2,1,0:T(8,128)} %so.1, f32[4,768,768]{2,1,0:T(8,128)} %get-tuple-element.9.u_in), custom_call_target="tpu_custom_call" | custom-call | tf_op jit(solution)/shard_map/fold_factors/pallas_call | solution.py:542

commit v5 on v4

--- a/solution.py
+++ b/solution.py
@@ -27,7 +27,8 @@
 CHUNKS = 8
 DEEP = 4
 ENTER = 18
-PUMPS = ENTER + COPIES
+LAG = (0, 2, 4, 5, 6, 7, 8, 9, 11, 12)
+PUMPS = ENTER + LAG[COPIES]
 DN0 = (((0,), (0,)), ((), ()))
 
 
@@ -409,7 +410,7 @@
             backward_first(5 - step)
 
         for k in range(1, COPIES + 1):
-            e = q - k
+            e = q - LAG[k]
 
             @pl.when(enters(e))
             def _(k=k, e=e):

time: 289 us -> 289 us (level)
  no operation moved by 1% of the time
where the time goes in v5:
time: 289 us; the launch traced here: 288 us
  Pallas kernels  288 us (100%)
    pallas_call x1, Pallas kernels, reduce_all(): pl.pallas_call(functools.partial(reduce_kernel, 1.0 / tokens), out_shape=...  263 us
    pallas_call x1, Pallas kernels, fold(): pl.pallas_call(functools.partial(fold_kernel, (1.0 - RHO) / tokens), out_...  24.8 us

profile of v5, /device:TPU:0, one launch (start us, length us, event | category | flops | bytes accessed | tf_op | source)
XLA Modules:
  0.0 288.3 jit_solution(8877504467201490334)
XLA Ops:
  0.6 262.8 %token_sums_reduced.1 = (f32[8,512,768]{2,1,0:T(8,128)}, f32[4,768,768]{2,1,0:T(8,128)}, bf16[3,4096,768]{2,1,0:T(8,128)(2,1)}, bf16[3,4096,768]{2,1,0:T(8,128)(2,1)}, bf16[3,4096,768]{2,1,0:T(8,128)(2,1)}) custom-call(bf16[4096,768]{1,0:T(8,128)(2,1)} %x.1, bf16[4096,768]{1,0:T(8,128)(2,1)} %dy.1, bf16[4,768,768]{2,1,0:T(8,128)(2,1)} %w.1, ...), custom_call_target="tpu_custom_call" | custom-call | flops 120795955200 | bytes 201326592 | tf_op jit(solution)/shard_map/token_sums_reduced/pallas_call | solution.py:477
  263.5 24.8 %fold_factors.1 = (f32[4,768,768]{2,1,0:T(8,128)}, f32[4,768,768]{2,1,0:T(8,128)}, f32[4,768,768]{2,1,0:T(8,128)}) custom-call(f32[8,512,768]{2,1,0:T(8,128)} %get-tuple-element.8.pa.ps, f32[8,512,768]{2,1,0:T(8,128)} %get-tuple-element.8.pa.ps, f32[4,768,768]{2,1,0:T(8,128)} %ao.1, f32[4,768,768]{2,1,0:T(8,128)} %so.1, f32[4,768,768]{2,1,0:T(8,128)} %get-tuple-element.9.u_in), custom_call_target="tpu_custom_call" | custom-call | tf_op jit(solution)/shard_map/fold_factors/pallas_call | solution.py:543
